TPU v7x, 32 devices: a whole 2x2x4 slice. The times are simulated.
32 devices in a mesh: gx: 8 (over z, core), gy: 4 (over y, x).
Axes of the slice: x: 2, y: 2, z: 4, core: 2. Of those that a mesh axis runs over, the one named last changes fastest.
Arguments:
- right_side: float32 [128, 128, 128], P('gx', 'gy'), may hold values from -6 to 6
- shift: float32 [128, 128, 128], P('gx', 'gy'), may hold values from 0.5 to 8
Outputs:
- solution_field: float32 [128, 128, 128], P('gx', 'gy')
- residual: float32 [128, 128, 128], P('gx', 'gy')
All inputs are finite; a program needn't handle non-finite values.
Results may differ from a plain program's by a relative error of at most 0.0003.
Values sent between devices are 32-bit elements; how exact they have to be, the bound alone decides.
A program may use at most 128 MiB of HBM per device.

v0:
```python
import functools

import jax
import jax.numpy as jnp
from jax import lax
from jax.experimental import pallas as pl
from jax.experimental.pallas import tpu as pltpu
from jax.sharding import PartitionSpec as P

MESH = pl.DeviceIdType.MESH
ROUNDS = 3
SWEEPS = 2
BOTTOM = 4
CENTER = 26.0
RELAX = 0.7
KEEP = 1.0 - RELAX
THETA = 1.0

SIDES = [(-1, 0), (1, 0), (0, -1), (0, 1)]
CORNERS = [(-1, -1), (-1, 1), (1, -1), (1, 1)]


def loop(count, body):
    def step(i, carry):
        body(i)
        return carry

    lax.fori_loop(0, count, step, 0)


def kernel(
    gx, gy, X, Y, Z,
    rhs, shf, out_x, out_r,
    g0, dA, wc0, e1, eA, eB, vbox, vext, wext,
    wc1, dd1, g1, e1b, eAb, eBb, wc2, e1c, eAc, eBc,
    pack, in_x, in_y, in_c, rx, ry, rc, gram,
    is_sem, ir_sem, s_sem, r_sem, gs_sem, gr_sem,
):
    n = gx * gy
    R = Y + 8
    n0, n1, n2 = X + 4, (X + 4) // 2, (X + 4) // 4
    ix, iy = lax.axis_index("gx"), lax.axis_index("gy")
    me = ix * gy + iy

    def there(dx, dy):
        ok = None
        for d, i, c in ((dx, ix, gx), (dy, iy, gy)):
            if d:
                here = (i > 0) if d < 0 else (i < c - 1)
                ok = here if ok is None else jnp.logical_and(ok, here)
        return ok

    def clear(refs):
        for ref in refs:
            lead = ref.shape[:-2] if len(ref.shape) == 3 else ref.shape[:-3]

            def body(i, ref=ref, lead=lead):
                at = (i,) if len(lead) == 1 else (i // lead[1], lax.rem(i, lead[1]))
                ref[at] = jnp.zeros(ref.shape[len(lead):], jnp.float32)

            loop(lead[0] if len(lead) == 1 else lead[0] * lead[1], body)

    clear((in_x, in_y, in_c, rx, ry, rc))
    barrier = pltpu.get_barrier_semaphore()

    @pl.loop(1, n)
    def _(d):
        other = lax.rem(me + d, n)
        pl.semaphore_signal(
            barrier, inc=1, device_id=(other // gy, lax.rem(other, gy)), device_id_type=MESH
        )

    clear((eA, eB, e1, vbox, g0, dA, eAb, eBb, e1b, eAc, eBc, e1c))

    pack[0, :, 0:2, :] = rhs[:, 0:2, :]
    pack[0, :, 2:4, :] = shf[:, 0:2, :]
    pack[1, :, 0:2, :] = rhs[:, Y - 2:Y, :]
    pack[1, :, 2:4, :] = shf[:, Y - 2:Y, :]
    pack[:, :, 4:8, :] = jnp.zeros((2, X, 4, Z), jnp.float32)

    pl.semaphore_wait(barrier, n - 1)

    def remote(src, dst, ss, rs, dx, dy):
        return pltpu.make_async_remote_copy(
            src_ref=src, dst_ref=dst, send_sem=ss, recv_sem=rs,
            device_id=(ix + dx, iy + dy), device_id_type=MESH,
        )

    def flip(k):
        return k ^ 1

    def first_copies():
        result = []
        for k, (dx, dy) in enumerate(SIDES):
            if dx:
                at = 0 if dx < 0 else X - 2
                for a, ref in enumerate((rhs, shf)):
                    result.append((dx, dy, ref.at[pl.ds(at, 2)], in_x.at[k ^ 1, a],
                                   2 * k + a, 2 * (k ^ 1) + a))
            else:
                result.append((dx, dy, pack.at[k - 2], in_y.at[(k - 2) ^ 1],
                               2 + k, 2 + (k ^ 1)))
        for k, (dx, dy) in enumerate(CORNERS):
            at = 0 if dx < 0 else X - 2
            row = 0 if dy < 0 else 1
            result.append((dx, dy, pack.at[row, pl.ds(at, 2)], in_c.at[3 - k], 6 + k, 6 + 3 - k))
        return result

    def back_copies(r):
        result = []
        box = vbox.at[r]
        for k, (dx, dy) in enumerate(SIDES):
            if dx:
                src = box.at[pl.ds(1 if dx < 0 else X, 5)]
                result.append((dx, dy, src, rx.at[r, k ^ 1], k, k ^ 1))
            else:
                src = box.at[pl.ds(1, n0), pl.ds(0 if dy < 0 else Y, 8)]
                result.append((dx, dy, src, ry.at[r, (k - 2) ^ 1], k, k ^ 1))
        for k, (dx, dy) in enumerate(CORNERS):
            src = box.at[pl.ds(1 if dx < 0 else X, 5), pl.ds(0 if dy < 0 else Y, 8)]
            result.append((dx, dy, src, rc.at[r, 3 - k], 4 + k, 4 + 3 - k))
        return result

    def start(copies, ss, rs):
        for dx, dy, src, dst, a, b in copies:
            @pl.when(there(dx, dy))
            def _(dx=dx, dy=dy, src=src, dst=dst, a=a, b=b):
                remote(src, dst, ss.at[a], rs.at[b], dx, dy).start()

    def arrive(copies, ss, rs):
        for dx, dy, src, dst, a, b in copies:
            @pl.when(there(-dx, -dy))
            def _(dx=dx, dy=dy, src=src, dst=dst, a=a, b=b):
                remote(src, dst, ss.at[a], rs.at[b], -dx, -dy).wait_recv()

    def leave(copies, ss, rs):
        for dx, dy, src, dst, a, b in copies:
            @pl.when(there(dx, dy))
            def _(dx=dx, dy=dy, src=src, dst=dst, a=a, b=b):
                remote(src, dst, ss.at[a], rs.at[b], dx, dy).wait_send()

    firsts = first_copies()
    start(firsts, is_sem, ir_sem)

    row = lax.broadcasted_iota(jnp.int32, (1, R, Z), 1)
    lane = lax.broadcasted_iota(jnp.int32, (1, R, Z), 2)

    g0[2:X + 2, 3:Y + 3, :] = rhs[...]
    dA[2:X + 2, 3:Y + 3, :] = shf[...]

    arrive(firsts, is_sem, ir_sem)
    for ref, a in ((g0, 0), (dA, 1)):
        ref[0:2, 3:Y + 3, :] = in_x[0, a]
        ref[X + 2:X + 4, 3:Y + 3, :] = in_x[1, a]
        ref[2:X + 2, 1:3, :] = in_y[0, :, 2 * a:2 * a + 2, :]
        ref[2:X + 2, Y + 3:Y + 5, :] = in_y[1, :, 2 * a:2 * a + 2, :]
        for k, (dx, dy) in enumerate(CORNERS):
            s = 0 if dx < 0 else X + 2
            t = 1 if dy < 0 else Y + 3
            ref[s:s + 2, t:t + 2, :] = in_c[k, :, 2 * a:2 * a + 2, :]

    in_box = jnp.logical_and(row >= 1, row <= Y + 4)
    relax = jnp.where(in_box, RELAX, 0.0).astype(jnp.float32)
    at_y = iy * Y + row - 3
    in_grid = jnp.where(
        jnp.logical_and(at_y >= 0, at_y < gy * Y), 1.0, 0.0
    ).astype(jnp.float32)

    def pair_sum(t, k):
        first = lax.rem(jnp.maximum(row - 1, 0) // k, 2) == 0
        t = t + jnp.where(first, pltpu.roll(t, R - k, 1), pltpu.roll(t, k, 1))
        low = lax.rem(lane // k, 2) == 0
        return t + jnp.where(low, pltpu.roll(t, Z - k, 2), pltpu.roll(t, k, 2))

    def cube(t, k):
        t = t + (pltpu.roll(t, k, 1) + pltpu.roll(t, R - k, 1))
        up = jnp.where(lane >= k, pltpu.roll(t, k, 2), 0.0)
        down = jnp.where(lane < Z - k, pltpu.roll(t, Z - k, 2), 0.0)
        return t + (up + down)

    def mean_shift(i):
        s = dA[pl.ds(2 * i, 2)]
        dd1[pl.ds(i, 1)] = pair_sum(s[0:1] + s[1:2], 1) * 0.125

    loop(n1, mean_shift)

    def diag0(i):
        s = dA[pl.ds(i, 1)]
        wc0[pl.ds(i, 1)] = relax / (CENTER + s)
        dA[pl.ds(i, 1)] = (CENTER + 1.0) + s

    loop(n0, diag0)

    def diag2(i):
        s = dd1[pl.ds(2 * i, 2)]
        s2 = pair_sum(s[0:1] + s[1:2], 2) * 0.125
        wc2[pl.ds(i, 1)] = relax / (CENTER + 16.0 * s2)

    loop(n2, diag2)

    def diag1(i):
        s = dd1[pl.ds(i, 1)]
        wc1[pl.ds(i, 1)] = relax / (CENTER + 4.0 * s)
        dd1[pl.ds(i, 1)] = (CENTER + 1.0) + 4.0 * s

    loop(n1, diag1)

    def scaled(dst, src, wc, count, ch):
        def body(i):
            at = i * ch
            dst[pl.ds(at + 1, ch)] = wc[pl.ds(at, ch)] * src[pl.ds(at, ch)]

        loop(count // ch, body)

    def sweep(dst, src, wg, wc, count, k, ch):
        def body(i):
            at = i * ch
            e = src[pl.ds(at, ch + 2)]
            mid = e[1:ch + 1]
            s = cube(e[0:ch] + mid + e[2:ch + 2], k)
            dst[pl.ds(at + 1, ch)] = (
                KEEP * mid + wg[pl.ds(at + 1, ch)] + wc[pl.ds(at, ch)] * (s - mid)
            )

        loop(count // ch, body)

    def down(dst, src, g, dp, count, k, ch):
        def body(i):
            at = i * ch
            e = src[pl.ds(at, ch + 2)]
            mid = e[1:ch + 1]
            s = cube(e[0:ch] + mid + e[2:ch + 2], k)
            left = g[pl.ds(at, ch)] - dp[pl.ds(at, ch)] * mid + s
            for h in range(ch // 2):
                both = left[2 * h:2 * h + 1] + left[2 * h + 1:2 * h + 2]
                dst[pl.ds(i * (ch // 2) + h, 1)] = 0.5 * pair_sum(both, k)

        loop(count // ch, body)

    def up(dst, src, count):
        def body(i):
            dst[pl.ds(2 * i + 1, 2)] = dst[pl.ds(2 * i + 1, 2)] + src[pl.ds(i + 1, 1)]

        loop(count // 2, body)

    def vcycle(dst, g, scratch):
        g2 = scratch
        scaled(e1, g, wc0, n0, 4)
        sweep(eA, e1, e1, wc0, n0, 1, 4)
        down(g1, eA, g, dA, n0, 1, 4)
        scaled(e1b, g1, wc1, n1, 2)
        sweep(eAb, e1b, e1b, wc1, n1, 2, 2)
        down(g2, eAb, g1, dd1, n1, 2, 2)
        scaled(e1c, g2, wc2, n2, n2)
        sweep(eAc, e1c, e1c, wc2, n2, 4, n2)
        sweep(eBc, eAc, e1c, wc2, n2, 4, n2)
        sweep(eAc, eBc, e1c, wc2, n2, 4, n2)
        up(eAb, eAc, n1)
        sweep(eBb, eAb, e1b, wc1, n1, 2, 2)
        sweep(eAb, eBb, e1b, wc1, n1, 2, 2)
        up(eA, eAb, n0)
        sweep(eB, eA, e1, wc0, n0, 1, 4)
        sweep(dst, eB, e1, wc0, n0, 1, 4)

    for r in range(ROUNDS):
        vcycle(vbox.at[r], g0 if r == 0 else wext.at[r - 1], eBc.at[pl.ds(1, n2)])
        copies = back_copies(r)
        ss, rs = s_sem.at[r], r_sem.at[r]
        start(copies, ss, rs)
        arrive(copies, ss, rs)

        v = vext.at[r]

        def take(i):
            v[pl.ds(2 * i, 2)] = vbox[r, pl.ds(2 * i, 2)]

        loop((n0 + 2) // 2, take)
        for k in range(2):
            s = 0 if k == 0 else X + 1
            v[s:s + 5] = v[s:s + 5] + rx[r, k]
        for k in range(2):
            t = 0 if k == 0 else Y
            v[1:n0 + 1, t:t + 8, :] = v[1:n0 + 1, t:t + 8, :] + ry[r, k]
        for k, (dx, dy) in enumerate(CORNERS):
            s = 0 if dx < 0 else X + 1
            t = 0 if dy < 0 else Y
            v[s:s + 5, t:t + 8, :] = v[s:s + 5, t:t + 8, :] + rc[r, k]

        def trim(i):
            t = v[pl.ds(2 * i, 2)] * in_grid
            if r:
                t = t - THETA * vext[r - 1, pl.ds(2 * i, 2)]
            v[pl.ds(2 * i, 2)] = t

        loop((n0 + 2) // 2, trim)

        @pl.when(ix == 0)
        def _():
            v[0:3] = jnp.zeros((3, R, Z), jnp.float32)

        @pl.when(ix == gx - 1)
        def _():
            v[X + 3:X + 6] = jnp.zeros((3, R, Z), jnp.float32)

        w = wext.at[r]

        def apply(i):
            at = i * 4
            e = v[pl.ds(at, 6)]
            mid = e[1:5]
            s = cube(e[0:4] + mid + e[2:6], 1)
            w[pl.ds(at, 4)] = in_grid * (dA[pl.ds(at, 4)] * mid - s)

        loop(n0 // 4, apply)

        @pl.when(ix == 0)
        def _():
            w[0:2] = jnp.zeros((2, R, Z), jnp.float32)

        @pl.when(ix == gx - 1)
        def _():
            w[X + 2:X + 4] = jnp.zeros((2, R, Z), jnp.float32)

    own = jnp.where(jnp.logical_and(row >= 3, row < Y + 3), 1.0, 0.0).astype(jnp.float32)

    def fold(t):
        t = t.reshape(R // 8, 8, Z)
        return jnp.sum(t, axis=0)

    def dots(i, sums):
        r0 = g0[pl.ds(i + 2, 1)]
        vs = [own * vext[k, pl.ds(i + 3, 1)] for k in range(ROUNDS)]
        ws = [wext[k, pl.ds(i + 2, 1)] for k in range(ROUNDS)]
        terms = [r0 * t for t in vs]
        terms += [vs[a] * ws[b] for a in range(ROUNDS) for b in range(a, ROUNDS)]
        return tuple(s + fold(t) for s, t in zip(sums, terms))

    zero = jnp.zeros((8, Z), jnp.float32)
    sums = lax.fori_loop(0, X, dots, (zero,) * 9)
    line = lax.broadcasted_iota(jnp.int32, (1, Z), 1)
    packed = jnp.zeros((1, Z), jnp.float32)
    for k, s in enumerate(sums):
        total = jnp.sum(jnp.sum(s, axis=0, keepdims=True), axis=1, keepdims=True)
        packed = jnp.where(line == k, total, packed)
    gram[me] = packed

    def gram_copy(d, back):
        other = lax.rem(me + d, n)
        slot = lax.rem(me + n - d, n) if back else me
        return pltpu.make_async_remote_copy(
            src_ref=gram.at[me], dst_ref=gram.at[slot],
            send_sem=gs_sem.at[d], recv_sem=gr_sem.at[slot],
            device_id=(other // gy, lax.rem(other, gy)), device_id_type=MESH,
        )

    @pl.loop(1, n)
    def _(d):
        gram_copy(d, False).start()

    @pl.loop(1, n)
    def _(d):
        gram_copy(d, True).wait_recv()

    total = jnp.sum(gram[...], axis=0)
    b0, b1, b2, g00, g01, g02, g11, g12, g22 = [
        jnp.broadcast_to(
            jnp.sum(jnp.where(line == k, total, 0.0), axis=1, keepdims=True), (1, Z)
        )
        for k in range(9)
    ]
    l1, l2 = g01 / g00, g02 / g00
    d1 = g11 - l1 * g01
    f12 = g12 - l1 * g02
    l3 = f12 / d1
    d2 = g22 - l2 * g02 - l3 * f12
    c1 = b1 - l1 * b0
    c2 = b2 - l2 * b0 - l3 * c1
    y2 = c2 / d2
    y1 = (c1 - f12 * y2) / d1
    y0 = (b0 - g01 * y1 - g02 * y2) / g00
    ys = [jnp.broadcast_to(t, (Y, Z)) for t in (y0, y1, y2)]

    def finish(i):
        x = ys[0] * vext[0, i + 3, 3:Y + 3, :]
        res = rhs[i] - ys[0] * wext[0, i + 2, 3:Y + 3, :]
        for k in range(1, ROUNDS):
            x = x + ys[k] * vext[k, i + 3, 3:Y + 3, :]
            res = res - ys[k] * wext[k, i + 2, 3:Y + 3, :]
        out_x[i] = x
        out_r[i] = res

    loop(X, finish)

    leave(firsts, is_sem, ir_sem)
    for r in range(ROUNDS):
        leave(back_copies(r), s_sem.at[r], r_sem.at[r])

    @pl.loop(1, n)
    def _(d):
        gram_copy(d, False).wait_send()


def on_device(gx, gy, right_side, shift):
    X, Y, Z = right_side.shape
    R = Y + 8
    n0, n1, n2 = X + 4, (X + 4) // 2, (X + 4) // 4
    n = gx * gy

    def field(*lead):
        return pltpu.VMEM(tuple(lead) + (R, Z), jnp.float32)

    scratch = [
        field(n0), field(n0), field(n0), field(n0 + 2), field(n0 + 2), field(n0 + 2),
        field(ROUNDS, n0 + 2), field(ROUNDS, n0 + 2), field(ROUNDS, n0),
        field(n1), field(n1), field(n1), field(n1 + 2), field(n1 + 2), field(n1 + 2),
        field(n2), field(n2 + 2), field(n2 + 2), field(n2 + 2),
        pltpu.VMEM((2, X, 8, Z), jnp.float32),
        pltpu.VMEM((2, 2, 2, Y, Z), jnp.float32),
        pltpu.VMEM((2, X, 8, Z), jnp.float32),
        pltpu.VMEM((4, 2, 8, Z), jnp.float32),
        field(ROUNDS, 2, 5),
        pltpu.VMEM((ROUNDS, 2, n0, 8, Z), jnp.float32),
        pltpu.VMEM((ROUNDS, 4, 5, 8, Z), jnp.float32),
        pltpu.VMEM((n, 1, Z), jnp.float32),
        pltpu.SemaphoreType.DMA((10,)),
        pltpu.SemaphoreType.DMA((10,)),
        pltpu.SemaphoreType.DMA((ROUNDS, 8)),
        pltpu.SemaphoreType.DMA((ROUNDS, 8)),
        pltpu.SemaphoreType.DMA((n,)),
        pltpu.SemaphoreType.DMA((n,)),
    ]
    shape = jax.ShapeDtypeStruct(right_side.shape, jnp.float32)
    return pl.pallas_call(
        functools.partial(kernel, gx, gy, X, Y, Z),
        out_shape=(shape, shape),
        in_specs=[pl.BlockSpec(memory_space=pltpu.VMEM)] * 2,
        out_specs=(pl.BlockSpec(memory_space=pltpu.VMEM),) * 2,
        scratch_shapes=scratch,
        compiler_params=pltpu.CompilerParams(
            collective_id=0, has_side_effects=True, vmem_limit_bytes=40 * 1024 * 1024
        ),
    )(right_side, shift)


def solution(mesh):
    spec = P("gx", "gy", None)
    return jax.shard_map(
        functools.partial(on_device, mesh.shape["gx"], mesh.shape["gy"]),
        mesh=mesh, in_specs=(spec, spec), out_specs=(spec, spec), check_vma=False,
    )
```

profile of v0, /device:TPU:0, one launch (start us, length us, event | category | flops | bytes accessed | tf_op | source)
XLA Modules:
  0.0 66.2 jit_solution(18031758089626090338)
XLA Ops:
  0.6 0.0 copy-start
  0.6 0.9 %copy-done = f32[16,32,128]{2,1,0:T(8,128)S(1)} copy-done((f32[16,32,128]{2,1,0:T(8,128)S(1)}, f32[16,32,128]{2,1,0:T(8,128)}, u32[]{:S(2)}) %copy-start) | copy-done | bytes 262168
  1.6 0.0 copy-start.1
  1.6 0.9 %copy-done.1 = f32[16,32,128]{2,1,0:T(8,128)S(1)} copy-done((f32[16,32,128]{2,1,0:T(8,128)S(1)}, f32[16,32,128]{2,1,0:T(8,128)}, u32[]{:S(2)}) %copy-start.1) | copy-done | bytes 262168
  2.5 62.2 %shard_map.41 = (f32[16,32,128]{2,1,0:T(8,128)S(1)}, f32[16,32,128]{2,1,0:T(8,128)S(1)}) custom-call(f32[16,32,128]{2,1,0:T(8,128)S(1)} %copy-done, f32[16,32,128]{2,1,0:T(8,128)S(1)} %copy-done.1), custom_call_target="tpu_custom_call" | custom-call | tf_op jit(solution)/shard_map/pallas_call | solution.py:433
  64.8 0.7 %copy.6 = f32[16,32,128]{2,1,0:T(8,128)} copy(f32[16,32,128]{2,1,0:T(8,128)S(1)} %get-tuple-element.4) | data formatting | bytes 524288
  65.5 0.7 %copy.7 = f32[16,32,128]{2,1,0:T(8,128)} copy(f32[16,32,128]{2,1,0:T(8,128)S(1)} %get-tuple-element.5) | data formatting | bytes 524288
Async XLA Ops:
  0.6 1.0 %copy-start = (f32[16,32,128]{2,1,0:T(8,128)S(1)}, f32[16,32,128]{2,1,0:T(8,128)}, u32[]{:S(2)}) copy-start(f32[16,32,128]{2,1,0:T(8,128)} %rhs.1) | copy-start | bytes 786436
  1.6 0.9 %copy-start.1 = (f32[16,32,128]{2,1,0:T(8,128)S(1)}, f32[16,32,128]{2,1,0:T(8,128)}, u32[]{:S(2)}) copy-start(f32[16,32,128]{2,1,0:T(8,128)} %shf.1) | copy-start | bytes 786436
where the time goes:
time: 66.4 us; the launch traced here: 66.2 us
  Pallas kernels  62.2 us (94%)
  local copies, waits for them, and re-layouts  3.3 us (5%)
    pallas_call x1, Pallas kernels, on_device(): pl.pallas_call(functools.partial(kernel, gx, gy, X, Y, Z), out_shape=(sha...  62.2 us
    unnamed x6, local copies, waits for them, and re-layouts  3.3 us

commit v1 on v0

v1 whole, which is shorter than its diff:
```python
import functools

import jax
import jax.numpy as jnp
from jax import lax
from jax.experimental import pallas as pl
from jax.experimental.pallas import tpu as pltpu
from jax.sharding import PartitionSpec as P

MESH = pl.DeviceIdType.MESH
ROUNDS = 3
SWEEPS = 2
BOTTOM = 4
CENTER = 26.0
RELAX = 0.7
KEEP = 1.0 - RELAX
THETA = 1.0
TOP = 8

SIDES = [(-1, 0), (1, 0), (0, -1), (0, 1)]
CORNERS = [(-1, -1), (-1, 1), (1, -1), (1, 1)]


def loop(count, body):
    def step(i, carry):
        body(i)
        return carry

    lax.fori_loop(0, count, step, 0)


def up8(k):
    return (k + 7) // 8 * 8


def kernel(
    gx, gy, X, Y, Z,
    rhs_hbm, shf_hbm, out_x, out_r,
    rhs, shf, g0, dA, wc0, cc0, e1, eA, eB, vbox, vext, wext,
    wc1, cc1, dd1, g1, e1b, eAb, eBb, wc2, cc2, g2, e1c, eAc, eBc,
    pack, in_x, in_y, in_c, ypack, rx, ry, rc, gram,
    ld_sem, is_sem, ir_sem, s_sem, r_sem, gs_sem, gr_sem,
):
    n = gx * gy
    R = Y + 8
    n0, n1, n2 = X + 4, (X + 4) // 2, (X + 4) // 4
    ix, iy = lax.axis_index("gx"), lax.axis_index("gy")
    me = ix * gy + iy
    rows = slice(TOP, TOP + R)

    def there(dx, dy):
        ok = None
        for d, i, c in ((dx, ix, gx), (dy, iy, gy)):
            if d:
                here = (i > 0) if d < 0 else (i < c - 1)
                ok = here if ok is None else jnp.logical_and(ok, here)
        return ok

    loads = [
        pltpu.make_async_copy(src, dst, ld_sem.at[k])
        for k, (src, dst) in enumerate(((rhs_hbm, rhs), (shf_hbm, shf)))
    ]
    for copy in loads:
        copy.start()
    barrier = pltpu.get_barrier_semaphore()

    @pl.loop(1, n)
    def _(d):
        other = lax.rem(me + d, n)
        pl.semaphore_signal(
            barrier, inc=1, device_id=(other // gy, lax.rem(other, gy)), device_id_type=MESH
        )

    for copy in loads:
        copy.wait()

    for side, at in ((0, 0), (1, Y - 2)):
        for p in range(X // 2):
            for q in range(2):
                pack[side, p, 4 * q:4 * q + 2, :] = rhs[2 * p + q, at:at + 2, :]
                pack[side, p, 4 * q + 2:4 * q + 4, :] = shf[2 * p + q, at:at + 2, :]

    pl.semaphore_wait(barrier, n - 1)

    def remote(item, ss, rs, dx, dy):
        return pltpu.make_async_remote_copy(
            src_ref=item[2], dst_ref=item[3], send_sem=ss.at[item[4]], recv_sem=rs.at[item[5]],
            device_id=(ix + dx, iy + dy), device_id_type=MESH,
        )

    def first_copies():
        result = []
        for k, (dx, dy) in enumerate(SIDES):
            if dx:
                at = 0 if dx < 0 else X - 2
                for a, ref in enumerate((rhs, shf)):
                    result.append((dx, dy, ref.at[pl.ds(at, 2)], in_x.at[k ^ 1, a],
                                   2 * k + a, 2 * (k ^ 1) + a))
            else:
                result.append((dx, dy, pack.at[k - 2], in_y.at[(k - 2) ^ 1],
                               2 + k, 2 + (k ^ 1)))
        for k, (dx, dy) in enumerate(CORNERS):
            at = 0 if dx < 0 else X // 2 - 1
            result.append((dx, dy, pack.at[0 if dy < 0 else 1, at], in_c.at[3 - k],
                           6 + k, 6 + 3 - k))
        return result

    def depth(r):
        return 5 if r + 1 < ROUNDS else 3

    def corner_rows(r, dx):
        d = depth(r)
        if dx < 0:
            return 0, up8(d * d), 0
        base = (n0 - d) * d
        return base // 8 * 8, up8(n0 * d), base % 8

    def back_copies(r):
        result = []
        d = depth(r)
        for k, (dx, dy) in enumerate(SIDES):
            if dx:
                at = 1 if dx < 0 else X + 5 - d
                src = vbox.at[r, pl.ds(at, d), pl.ds(TOP, R)]
                result.append((dx, dy, src, rx.at[r, k ^ 1, pl.ds(0, d)], k, k ^ 1))
            else:
                tall = up8(n0 * d)
                result.append((dx, dy, ypack.at[r, k - 2, pl.ds(0, tall)],
                               ry.at[r, (k - 2) ^ 1, pl.ds(0, tall)], k, k ^ 1))
        for k, (dx, dy) in enumerate(CORNERS):
            lo, hi, _ = corner_rows(r, dx)
            src = ypack.at[r, 0 if dy < 0 else 1, pl.ds(lo, hi - lo)]
            result.append((dx, dy, src, rc.at[r, 3 - k, pl.ds(0, hi - lo)], 4 + k, 4 + 3 - k))
        return result

    def start(copies, ss, rs):
        for item in copies[::-1]:
            dx, dy = item[:2]

            @pl.when(there(dx, dy))
            def _(item=item, dx=dx, dy=dy):
                remote(item, ss, rs, dx, dy).start()

    def arrive(copies, ss, rs, use):
        for item in copies:
            dx, dy = -item[0], -item[1]

            @pl.when(there(dx, dy))
            def _(item=item, dx=dx, dy=dy):
                remote(item, ss, rs, dx, dy).wait_recv()
                use(dx, dy, item[3], item[5])

    def leave(copies, ss, rs):
        for item in copies:
            dx, dy = item[:2]

            @pl.when(there(dx, dy))
            def _(item=item, dx=dx, dy=dy):
                remote(item, ss, rs, dx, dy).wait_send()

    firsts = first_copies()
    start(firsts, is_sem, ir_sem)

    for ref in (eA, eB, e1, vbox, vext, g0, dA, eAb, eBb, e1b, eAc, eBc, e1c):
        lead = ref.shape[:-2]

        def clear(i, ref=ref, lead=lead):
            at = (i,) if len(lead) == 1 else (i // lead[1], lax.rem(i, lead[1]))
            ref[at] = jnp.zeros(ref.shape[-2:], jnp.float32)

        loop(lead[0] if len(lead) == 1 else lead[0] * lead[1], clear)

    row = lax.broadcasted_iota(jnp.int32, (1, R, Z), 1)
    lane = lax.broadcasted_iota(jnp.int32, (1, R, Z), 2)

    g0[2:X + 2, 3:Y + 3, :] = rhs[...]
    dA[2:X + 2, 3:Y + 3, :] = shf[...]

    def use_first(dx, dy, got, slot):
        s = 0 if dx < 0 else X + 2
        t = 1 if dy < 0 else Y + 3
        if dy == 0:
            (g0, dA)[slot % 2][s:s + 2, 3:Y + 3, :] = got[...]
            return
        for a, ref in enumerate((g0, dA)):
            if dx == 0:
                for i in range(X):
                    q = 4 * (i % 2) + 2 * a
                    ref[2 + i, t:t + 2, :] = got[i // 2, q:q + 2, :]
            else:
                for q in range(2):
                    p = 4 * q + 2 * a
                    ref[s + q, t:t + 2, :] = got[p:p + 2, :]

    arrive(firsts, is_sem, ir_sem, use_first)

    in_box = jnp.logical_and(row >= 1, row <= Y + 4)
    relax = jnp.where(in_box, RELAX, 0.0).astype(jnp.float32)
    at_y = iy * Y + row - 3
    in_grid = jnp.where(
        jnp.logical_and(at_y >= 0, at_y < gy * Y), 1.0, 0.0
    ).astype(jnp.float32)

    def pair_sum(t, k):
        first = lax.rem(jnp.maximum(row - 1, 0) // k, 2) == 0
        t = t + jnp.where(first, pltpu.roll(t, R - k, 1), pltpu.roll(t, k, 1))
        low = lax.rem(lane // k, 2) == 0
        return t + jnp.where(low, pltpu.roll(t, Z - k, 2), pltpu.roll(t, k, 2))

    def cube(src, at, ch, k):
        got = src[pl.ds(at, ch + 2), rows, :]
        t = got + (
            src[pl.ds(at, ch + 2), TOP - k:TOP - k + R, :]
            + src[pl.ds(at, ch + 2), TOP + k:TOP + k + R, :]
        )
        t = t[0:ch] + t[1:ch + 1] + t[2:ch + 2]
        up = jnp.where(lane >= k, pltpu.roll(t, k, 2), 0.0)
        down = jnp.where(lane < Z - k, pltpu.roll(t, Z - k, 2), 0.0)
        return got[1:ch + 1], t + (up + down)

    def mean_shift(i):
        s = dA[pl.ds(2 * i, 2)]
        dd1[pl.ds(i, 1)] = pair_sum(s[0:1] + s[1:2], 1) * 0.125

    loop(n1, mean_shift)

    def weights(wc, cc, dp, count, values):
        def body(i):
            d = CENTER + values(i)
            w = relax / d
            wc[pl.ds(i, 1)] = w
            cc[pl.ds(i, 1)] = KEEP - w
            if dp is not None:
                dp[pl.ds(i, 1)] = d + 1.0

        loop(count, body)

    def mean_second(i):
        s = dd1[pl.ds(2 * i, 2)]
        return 16.0 * (pair_sum(s[0:1] + s[1:2], 2) * 0.125)

    weights(wc0, cc0, dA, n0, lambda i: dA[pl.ds(i, 1)])
    weights(wc2, cc2, None, n2, mean_second)
    weights(wc1, cc1, dd1, n1, lambda i: 4.0 * dd1[pl.ds(i, 1)])

    def scaled(dst, src, wc, count, ch):
        def body(i):
            at = i * ch
            dst[pl.ds(at + 1, ch), rows, :] = wc[pl.ds(at, ch)] * src[pl.ds(at, ch)]

        loop(count // ch, body)

    def sweep(dst, src, wg, wc, cc, count, k, ch):
        def body(i):
            at = i * ch
            mid, s = cube(src, at, ch, k)
            base = mid if wg is src else wg[pl.ds(at + 1, ch), rows, :]
            dst[pl.ds(at + 1, ch), rows, :] = (
                cc[pl.ds(at, ch)] * mid + base + wc[pl.ds(at, ch)] * s
            )

        loop(count // ch, body)

    def down(dst, src, g, dp, count, k, ch):
        def body(i):
            at = i * ch
            mid, s = cube(src, at, ch, k)
            left = g[pl.ds(at, ch)] - dp[pl.ds(at, ch)] * mid + s
            both = [left[2 * h:2 * h + 1] + left[2 * h + 1:2 * h + 2] for h in range(ch // 2)]
            both = jnp.concatenate(both, axis=0)
            dst[pl.ds(i * (ch // 2), ch // 2)] = 0.5 * pair_sum(both, k)

        loop(count // ch, body)

    def up(dst, src, count):
        def body(i):
            dst[pl.ds(2 * i + 1, 2), rows, :] = (
                dst[pl.ds(2 * i + 1, 2), rows, :] + src[pl.ds(i + 1, 1), rows, :]
            )

        loop(count // 2, body)

    h0 = n0 // 2

    def vcycle(dst, g):
        sweep(eA, e1, e1, wc0, cc0, n0, 1, h0)
        down(g1, eA, g, dA, n0, 1, h0)
        scaled(e1b, g1, wc1, n1, n1)
        sweep(eAb, e1b, e1b, wc1, cc1, n1, 2, n1)
        down(g2, eAb, g1, dd1, n1, 2, n1)
        scaled(e1c, g2, wc2, n2, n2)
        sweep(eAc, e1c, e1c, wc2, cc2, n2, 4, n2)
        for turn in range(BOTTOM - 2):
            a, b = (eBc, eAc) if turn % 2 == 0 else (eAc, eBc)
            sweep(a, b, e1c, wc2, cc2, n2, 4, n2)
        up(eAb, eAc, n1)
        sweep(eBb, eAb, e1b, wc1, cc1, n1, 2, n1)
        sweep(eAb, eBb, e1b, wc1, cc1, n1, 2, n1)
        up(eA, eAb, n0)
        sweep(eB, eA, e1, wc0, cc0, n0, 1, h0)
        sweep(dst, eB, e1, wc0, cc0, n0, 1, h0)

    own = jnp.where(jnp.logical_and(row >= 3, row < Y + 3), 1.0, 0.0).astype(jnp.float32)

    def dots(r):
        ch = 4

        def body(i, sums):
            w = own * wext[r, pl.ds(ch * i + 2, ch)]
            terms = [own * g0[pl.ds(ch * i + 2, ch)] * vext[r, pl.ds(ch * i + 3, ch), rows, :]]
            terms += [vext[a, pl.ds(ch * i + 3, ch), rows, :] * w for a in range(r + 1)]
            return tuple(
                s + jnp.sum(t.reshape(ch * R // 8, 8, Z), axis=0) for s, t in zip(sums, terms)
            )

        zero = jnp.zeros((8, Z), jnp.float32)
        return lax.fori_loop(0, X // ch, body, (zero,) * (r + 2))

    scaled(e1, g0, wc0, n0, 4)
    sums = []
    for r in range(ROUNDS):
        vcycle(vbox.at[r], g0 if r == 0 else wext.at[r - 1])
        d = depth(r)
        for i in range(n0):
            ypack[r, 0, d * i:d * i + d, :] = vbox[r, i + 1, TOP + 1:TOP + 1 + d, :]
            ypack[r, 1, d * i:d * i + d, :] = vbox[r, i + 1, TOP + Y + 5 - d:TOP + Y + 5, :]
        copies = back_copies(r)
        ss, rs = s_sem.at[r], r_sem.at[r]
        start(copies, ss, rs)

        v = vext.at[r]

        def take(i):
            at = pl.ds(2 * i, 2)
            t = vbox[r, at, rows, :] * in_grid
            if r:
                t = t - THETA * vext[r - 1, at, rows, :]
            v[at, rows, :] = t

        loop((n0 + 2) // 2, take)
        if r:
            sums.append(dots(r - 1))

        def use_back(dx, dy, got, slot):
            s = 5 - d if dx < 0 else X + 1
            t = TOP + 5 - d if dy < 0 else TOP + Y + 1
            if dy == 0:
                v[s:s + d, rows, :] = v[s:s + d, rows, :] + got[...] * in_grid
                return
            skip = 0 if dx == 0 else corner_rows(r, -dx)[2]
            if dx == 0:
                s = 1
            for j in range(n0 if dx == 0 else d):
                v[s + j, t:t + d, :] = (
                    v[s + j, t:t + d, :] + got[skip + d * j:skip + d * j + d, :]
                )

        arrive(copies, ss, rs, use_back)

        @pl.when(ix == 0)
        def _():
            v[0:3, rows, :] = jnp.zeros((3, R, Z), jnp.float32)

        @pl.when(ix == gx - 1)
        def _():
            v[X + 3:X + 6, rows, :] = jnp.zeros((3, R, Z), jnp.float32)

        w = wext.at[r]
        last = r + 1 == ROUNDS

        def apply(i):
            ch = X // 2 if last else h0
            at = i * ch + (2 if last else 0)
            mid, s = cube(v, at, ch, 1)
            t = in_grid * (dA[pl.ds(at, ch)] * mid - s)
            w[pl.ds(at, ch)] = t
            if not last:
                e1[pl.ds(at + 1, ch), rows, :] = wc0[pl.ds(at, ch)] * t

        loop(2, apply)

        if not last:
            for edge, at in ((0, 0), (gx - 1, X + 2)):
                @pl.when(ix == edge)
                def _(at=at):
                    w[at:at + 2] = jnp.zeros((2, R, Z), jnp.float32)
                    e1[at + 1:at + 3, rows, :] = jnp.zeros((2, R, Z), jnp.float32)

    sums.append(dots(ROUNDS - 1))
    flat = [t for group in sums for t in group]
    line = lax.broadcasted_iota(jnp.int32, (1, Z), 1)
    packed = jnp.zeros((1, Z), jnp.float32)
    for k, s in enumerate(flat):
        total = jnp.sum(jnp.sum(s, axis=0, keepdims=True), axis=1, keepdims=True)
        packed = jnp.where(line == k, total, packed)
    gram[me] = packed

    def gram_copy(d, back):
        other = lax.rem(me + d, n)
        slot = lax.rem(me + n - d, n) if back else me
        return pltpu.make_async_remote_copy(
            src_ref=gram.at[me], dst_ref=gram.at[slot],
            send_sem=gs_sem.at[d], recv_sem=gr_sem.at[slot],
            device_id=(other // gy, lax.rem(other, gy)), device_id_type=MESH,
        )

    @pl.loop(1, n)
    def _(d):
        gram_copy(d, False).start()

    @pl.loop(1, n)
    def _(d):
        gram_copy(d, True).wait_recv()

    total = jnp.sum(gram[...], axis=0)
    b0, g00, b1, g01, g11, b2, g02, g12, g22 = [
        jnp.broadcast_to(
            jnp.sum(jnp.where(line == k, total, 0.0), axis=1, keepdims=True), (1, Z)
        )
        for k in range(9)
    ]
    l1, l2 = g01 / g00, g02 / g00
    d1 = g11 - l1 * g01
    f12 = g12 - l1 * g02
    l3 = f12 / d1
    d2 = g22 - l2 * g02 - l3 * f12
    c1 = b1 - l1 * b0
    c2 = b2 - l2 * b0 - l3 * c1
    y2 = c2 / d2
    y1 = (c1 - f12 * y2) / d1
    y0 = (b0 - g01 * y1 - g02 * y2) / g00
    ys = [jnp.broadcast_to(t, (Y, Z)) for t in (y0, y1, y2)]

    def finish(i):
        x = ys[0] * vext[0, i + 3, TOP + 3:TOP + Y + 3, :]
        res = rhs[i] - ys[0] * wext[0, i + 2, 3:Y + 3, :]
        for k in range(1, ROUNDS):
            x = x + ys[k] * vext[k, i + 3, TOP + 3:TOP + Y + 3, :]
            res = res - ys[k] * wext[k, i + 2, 3:Y + 3, :]
        out_x[i] = x
        out_r[i] = res

    loop(X, finish)

    leave(firsts, is_sem, ir_sem)
    for r in range(ROUNDS):
        leave(back_copies(r), s_sem.at[r], r_sem.at[r])

    @pl.loop(1, n)
    def _(d):
        gram_copy(d, False).wait_send()


def on_device(gx, gy, right_side, shift):
    X, Y, Z = right_side.shape
    R = Y + 8
    n0, n1, n2 = X + 4, (X + 4) // 2, (X + 4) // 4
    n = gx * gy

    def field(*lead):
        return pltpu.VMEM(tuple(lead) + (R, Z), jnp.float32)

    def tall(*lead):
        return pltpu.VMEM(tuple(lead) + (R + 2 * TOP, Z), jnp.float32)

    def plain(*shape):
        return pltpu.VMEM(tuple(shape) + (Z,), jnp.float32)

    packed = up8(n0 * 5)
    scratch = [
        plain(X, Y), plain(X, Y),
        field(n0), field(n0), field(n0), field(n0), tall(n0 + 2), tall(n0 + 2), tall(n0 + 2),
        tall(ROUNDS, n0 + 2), tall(ROUNDS, n0 + 2), field(ROUNDS, n0),
        field(n1), field(n1), field(n1), field(n1), tall(n1 + 2), tall(n1 + 2), tall(n1 + 2),
        field(n2), field(n2), field(n2), tall(n2 + 2), tall(n2 + 2), tall(n2 + 2),
        plain(2, X // 2, 8), plain(2, 2, 2, Y), plain(2, X // 2, 8), plain(4, 8),
        plain(ROUNDS, 2, packed), field(ROUNDS, 2, 5), plain(ROUNDS, 2, packed),
        plain(ROUNDS, 4, 32), plain(n, 1),
        pltpu.SemaphoreType.DMA((2,)),
        pltpu.SemaphoreType.DMA((10,)),
        pltpu.SemaphoreType.DMA((10,)),
        pltpu.SemaphoreType.DMA((ROUNDS, 8)),
        pltpu.SemaphoreType.DMA((ROUNDS, 8)),
        pltpu.SemaphoreType.DMA((n,)),
        pltpu.SemaphoreType.DMA((n,)),
    ]
    shape = jax.ShapeDtypeStruct(right_side.shape, jnp.float32)
    return pl.pallas_call(
        functools.partial(kernel, gx, gy, X, Y, Z),
        out_shape=(shape, shape),
        in_specs=[pl.BlockSpec(memory_space=pltpu.HBM)] * 2,
        out_specs=(pl.BlockSpec(memory_space=pltpu.VMEM),) * 2,
        scratch_shapes=scratch,
        compiler_params=pltpu.CompilerParams(
            collective_id=0, has_side_effects=True, vmem_limit_bytes=40 * 1024 * 1024
        ),
    )(right_side, shift)


def solution(mesh):
    spec = P("gx", "gy", None)
    return jax.shard_map(
        functools.partial(on_device, mesh.shape["gx"], mesh.shape["gy"]),
        mesh=mesh, in_specs=(spec, spec), out_specs=(spec, spec), check_vma=False,
    )
```

time: 66.4 us -> 46 us (0.69)
  Pallas kernels: 62.2 us -> 41.9 us
    pallas_call x1, Pallas kernels: 62.2 us -> 41.9 us  [on_device(): pl.pallas_call(functools.partial(kernel, gx, gy, X, Y, Z), out_shape=(sha...]
where the time goes in v1:
time: 46 us; the launch traced here: 45.8 us
  Pallas kernels  41.9 us (91%)
  local copies, waits for them, and re-layouts  3.3 us (7%)
  between operations  0.65 us (1%)
    pallas_call x1, Pallas kernels, on_device(): pl.pallas_call(functools.partial(kernel, gx, gy, X, Y, Z), out_shape=(sha...  41.9 us
    unnamed x6, local copies, waits for them, and re-layouts  3.3 us

profile of v1, /device:TPU:0, one launch (start us, length us, event | category | flops | bytes accessed | tf_op | source)
XLA Modules:
  0.0 45.8 jit_solution(12945158016506689228)
XLA Ops:
  0.6 0.0 copy-start
  0.6 0.9 %copy-done = f32[16,32,128]{2,1,0:T(8,128)S(1)} copy-done((f32[16,32,128]{2,1,0:T(8,128)S(1)}, f32[16,32,128]{2,1,0:T(8,128)}, u32[]{:S(2)}) %copy-start) | copy-done | bytes 262168
  1.6 0.0 copy-start.1
  1.6 0.9 %copy-done.1 = f32[16,32,128]{2,1,0:T(8,128)S(1)} copy-done((f32[16,32,128]{2,1,0:T(8,128)S(1)}, f32[16,32,128]{2,1,0:T(8,128)}, u32[]{:S(2)}) %copy-start.1) | copy-done | bytes 262168
  2.5 41.9 %shard_map.41 = (f32[16,32,128]{2,1,0:T(8,128)S(1)}, f32[16,32,128]{2,1,0:T(8,128)S(1)}) custom-call(f32[16,32,128]{2,1,0:T(8,128)S(1)} %copy-done, f32[16,32,128]{2,1,0:T(8,128)S(1)} %copy-done.1), custom_call_target="tpu_custom_call" | custom-call | tf_op jit(solution)/shard_map/pallas_call | solution.py:488
  44.4 0.7 %copy.6 = f32[16,32,128]{2,1,0:T(8,128)} copy(f32[16,32,128]{2,1,0:T(8,128)S(1)} %get-tuple-element.4) | data formatting | bytes 524288
  45.1 0.7 %copy.7 = f32[16,32,128]{2,1,0:T(8,128)} copy(f32[16,32,128]{2,1,0:T(8,128)S(1)} %get-tuple-element.5) | data formatting | bytes 524288
Async XLA Ops:
  0.6 1.0 %copy-start = (f32[16,32,128]{2,1,0:T(8,128)S(1)}, f32[16,32,128]{2,1,0:T(8,128)}, u32[]{:S(2)}) copy-start(f32[16,32,128]{2,1,0:T(8,128)} %rhs_hbm.1) | copy-start | bytes 786436
  1.6 0.9 %copy-start.1 = (f32[16,32,128]{2,1,0:T(8,128)S(1)}, f32[16,32,128]{2,1,0:T(8,128)}, u32[]{:S(2)}) copy-start(f32[16,32,128]{2,1,0:T(8,128)} %shf_hbm.1) | copy-start | bytes 786436

commit v2 on v1

--- a/solution.py
+++ b/solution.py
@@ -16,6 +16,7 @@
 KEEP = 1.0 - RELAX
 THETA = 1.0
 TOP = 8
+VMEM_GRANT = 41943040
 
 SIDES = [(-1, 0), (1, 0), (0, -1), (0, 1)]
 CORNERS = [(-1, -1), (-1, 1), (1, -1), (1, 1)]
@@ -64,12 +65,22 @@
         copy.start()
     barrier = pltpu.get_barrier_semaphore()
 
-    @pl.loop(1, n)
-    def _(d):
-        other = lax.rem(me + d, n)
+    xs = [ix] + [jnp.where(ix + k < gx, ix + k, ix + k - gx) for k in range(1, gx)]
+    ys_at = [iy] + [jnp.where(iy + k < gy, iy + k, iy + k - gy) for k in range(1, gy)]
+    others = [(a, b) for a in range(gx) for b in range(gy)][1:]
+    for a, b in others:
         pl.semaphore_signal(
-            barrier, inc=1, device_id=(other // gy, lax.rem(other, gy)), device_id_type=MESH
+            barrier, inc=1, device_id=(xs[a], ys_at[b]), device_id_type=MESH
         )
+
+    for ref in (eA, eB, e1, vbox, vext, g0, dA, eAb, eBb, e1b, eAc, eBc, e1c):
+        lead = ref.shape[:-2]
+
+        def clear(i, ref=ref, lead=lead):
+            at = (i,) if len(lead) == 1 else (i // lead[1], lax.rem(i, lead[1]))
+            ref[at] = jnp.zeros(ref.shape[-2:], jnp.float32)
+
+        loop(lead[0] if len(lead) == 1 else lead[0] * lead[1], clear)
 
     for copy in loads:
         copy.wait()
@@ -79,6 +90,9 @@
             for q in range(2):
                 pack[side, p, 4 * q:4 * q + 2, :] = rhs[2 * p + q, at:at + 2, :]
                 pack[side, p, 4 * q + 2:4 * q + 4, :] = shf[2 * p + q, at:at + 2, :]
+
+    g0[2:X + 2, 3:Y + 3, :] = rhs[...]
+    dA[2:X + 2, 3:Y + 3, :] = shf[...]
 
     pl.semaphore_wait(barrier, n - 1)
 
@@ -161,20 +175,9 @@
     firsts = first_copies()
     start(firsts, is_sem, ir_sem)
 
-    for ref in (eA, eB, e1, vbox, vext, g0, dA, eAb, eBb, e1b, eAc, eBc, e1c):
-        lead = ref.shape[:-2]
-
-        def clear(i, ref=ref, lead=lead):
-            at = (i,) if len(lead) == 1 else (i // lead[1], lax.rem(i, lead[1]))
-            ref[at] = jnp.zeros(ref.shape[-2:], jnp.float32)
-
-        loop(lead[0] if len(lead) == 1 else lead[0] * lead[1], clear)
-
     row = lax.broadcasted_iota(jnp.int32, (1, R, Z), 1)
     lane = lax.broadcasted_iota(jnp.int32, (1, R, Z), 2)
-
-    g0[2:X + 2, 3:Y + 3, :] = rhs[...]
-    dA[2:X + 2, 3:Y + 3, :] = shf[...]
+    flat_lane = lax.broadcasted_iota(jnp.int32, (R, Z), 1)
 
     def use_first(dx, dy, got, slot):
         s = 0 if dx < 0 else X + 2
@@ -208,32 +211,37 @@
         return t + jnp.where(low, pltpu.roll(t, Z - k, 2), pltpu.roll(t, k, 2))
 
     def cube(src, at, ch, k):
-        got = src[pl.ds(at, ch + 2), rows, :]
-        t = got + (
-            src[pl.ds(at, ch + 2), TOP - k:TOP - k + R, :]
-            + src[pl.ds(at, ch + 2), TOP + k:TOP + k + R, :]
-        )
-        t = t[0:ch] + t[1:ch + 1] + t[2:ch + 2]
-        up = jnp.where(lane >= k, pltpu.roll(t, k, 2), 0.0)
-        down = jnp.where(lane < Z - k, pltpu.roll(t, Z - k, 2), 0.0)
-        return got[1:ch + 1], t + (up + down)
+        last = []
+        for j in range(ch + 2):
+            got = src[at + j, rows, :]
+            t = got + (src[at + j, TOP - k:TOP - k + R, :] + src[at + j, TOP + k:TOP + k + R, :])
+            last.append((got, t))
+            if j >= 2:
+                t = last[0][1] + last[1][1] + last[2][1]
+                up = jnp.where(flat_lane >= k, pltpu.roll(t, k, 1), 0.0)
+                down = jnp.where(flat_lane < Z - k, pltpu.roll(t, Z - k, 1), 0.0)
+                yield j - 2, last[1][0], t + (up + down)
+                last = last[1:]
 
     def mean_shift(i):
-        s = dA[pl.ds(2 * i, 2)]
-        dd1[pl.ds(i, 1)] = pair_sum(s[0:1] + s[1:2], 1) * 0.125
-
-    loop(n1, mean_shift)
+        for j in range(5):
+            s = dA[pl.ds(10 * i + 2 * j, 2)]
+            dd1[pl.ds(5 * i + j, 1)] = pair_sum(s[0:1] + s[1:2], 1) * 0.125
+
+    loop(n1 // 5, mean_shift)
 
     def weights(wc, cc, dp, count, values):
         def body(i):
-            d = CENTER + values(i)
-            w = relax / d
-            wc[pl.ds(i, 1)] = w
-            cc[pl.ds(i, 1)] = KEEP - w
-            if dp is not None:
-                dp[pl.ds(i, 1)] = d + 1.0
-
-        loop(count, body)
+            for j in range(5):
+                at = pl.ds(5 * i + j, 1)
+                d = CENTER + values(5 * i + j)
+                w = relax / d
+                wc[at] = w
+                cc[at] = KEEP - w
+                if dp is not None:
+                    dp[at] = d + 1.0
+
+        loop(count // 5, body)
 
     def mean_second(i):
         s = dd1[pl.ds(2 * i, 2)]
@@ -253,22 +261,20 @@
     def sweep(dst, src, wg, wc, cc, count, k, ch):
         def body(i):
             at = i * ch
-            mid, s = cube(src, at, ch, k)
-            base = mid if wg is src else wg[pl.ds(at + 1, ch), rows, :]
-            dst[pl.ds(at + 1, ch), rows, :] = (
-                cc[pl.ds(at, ch)] * mid + base + wc[pl.ds(at, ch)] * s
-            )
+            for j, mid, s in cube(src, at, ch, k):
+                base = mid if wg is src else wg[at + j + 1, rows, :]
+                dst[at + j + 1, rows, :] = cc[at + j] * mid + base + wc[at + j] * s
 
         loop(count // ch, body)
 
     def down(dst, src, g, dp, count, k, ch):
         def body(i):
             at = i * ch
-            mid, s = cube(src, at, ch, k)
-            left = g[pl.ds(at, ch)] - dp[pl.ds(at, ch)] * mid + s
-            both = [left[2 * h:2 * h + 1] + left[2 * h + 1:2 * h + 2] for h in range(ch // 2)]
-            both = jnp.concatenate(both, axis=0)
-            dst[pl.ds(i * (ch // 2), ch // 2)] = 0.5 * pair_sum(both, k)
+            for j, mid, s in cube(src, at, ch, k):
+                left = g[at + j] - dp[at + j] * mid + s
+                if j % 2:
+                    dst[i * (ch // 2) + j // 2] = 0.5 * pair_sum((held + left)[None], k)[0]
+                held = left
 
         loop(count // ch, body)
 
@@ -371,11 +377,11 @@
         def apply(i):
             ch = X // 2 if last else h0
             at = i * ch + (2 if last else 0)
-            mid, s = cube(v, at, ch, 1)
-            t = in_grid * (dA[pl.ds(at, ch)] * mid - s)
-            w[pl.ds(at, ch)] = t
-            if not last:
-                e1[pl.ds(at + 1, ch), rows, :] = wc0[pl.ds(at, ch)] * t
+            for j, mid, s in cube(v, at, ch, 1):
+                t = in_grid[0] * (dA[at + j] * mid - s)
+                w[at + j] = t
+                if not last:
+                    e1[at + j + 1, rows, :] = wc0[at + j] * t
 
         loop(2, apply)
 
@@ -395,22 +401,21 @@
         packed = jnp.where(line == k, total, packed)
     gram[me] = packed
 
-    def gram_copy(d, back):
-        other = lax.rem(me + d, n)
-        slot = lax.rem(me + n - d, n) if back else me
+    def gram_copy(k, back):
+        a, b = others[k]
+        slot = me
+        if back:
+            slot = xs[(gx - a) % gx] * gy + ys_at[(gy - b) % gy]
         return pltpu.make_async_remote_copy(
             src_ref=gram.at[me], dst_ref=gram.at[slot],
-            send_sem=gs_sem.at[d], recv_sem=gr_sem.at[slot],
-            device_id=(other // gy, lax.rem(other, gy)), device_id_type=MESH,
+            send_sem=gs_sem.at[k], recv_sem=gr_sem.at[slot],
+            device_id=(xs[a], ys_at[b]), device_id_type=MESH,
         )
 
-    @pl.loop(1, n)
-    def _(d):
-        gram_copy(d, False).start()
-
-    @pl.loop(1, n)
-    def _(d):
-        gram_copy(d, True).wait_recv()
+    for k in range(n - 1)[::-1]:
+        gram_copy(k, False).start()
+    for k in range(n - 1):
+        gram_copy(k, True).wait_recv()
 
     total = jnp.sum(gram[...], axis=0)
     b0, g00, b1, g01, g11, b2, g02, g12, g22 = [
@@ -432,23 +437,24 @@
     ys = [jnp.broadcast_to(t, (Y, Z)) for t in (y0, y1, y2)]
 
     def finish(i):
-        x = ys[0] * vext[0, i + 3, TOP + 3:TOP + Y + 3, :]
-        res = rhs[i] - ys[0] * wext[0, i + 2, 3:Y + 3, :]
-        for k in range(1, ROUNDS):
-            x = x + ys[k] * vext[k, i + 3, TOP + 3:TOP + Y + 3, :]
-            res = res - ys[k] * wext[k, i + 2, 3:Y + 3, :]
-        out_x[i] = x
-        out_r[i] = res
-
-    loop(X, finish)
+        for j in range(4):
+            p = 4 * i + j
+            x = ys[0] * vext[0, p + 3, TOP + 3:TOP + Y + 3, :]
+            res = rhs[p] - ys[0] * wext[0, p + 2, 3:Y + 3, :]
+            for k in range(1, ROUNDS):
+                x = x + ys[k] * vext[k, p + 3, TOP + 3:TOP + Y + 3, :]
+                res = res - ys[k] * wext[k, p + 2, 3:Y + 3, :]
+            out_x[p] = x
+            out_r[p] = res
+
+    loop(X // 4, finish)
 
     leave(firsts, is_sem, ir_sem)
     for r in range(ROUNDS):
         leave(back_copies(r), s_sem.at[r], r_sem.at[r])
 
-    @pl.loop(1, n)
-    def _(d):
-        gram_copy(d, False).wait_send()
+    for k in range(n - 1):
+        gram_copy(k, False).wait_send()
 
 
 def on_device(gx, gy, right_side, shift):
@@ -492,7 +498,7 @@
         out_specs=(pl.BlockSpec(memory_space=pltpu.VMEM),) * 2,
         scratch_shapes=scratch,
         compiler_params=pltpu.CompilerParams(
-            collective_id=0, has_side_effects=True, vmem_limit_bytes=40 * 1024 * 1024
+            collective_id=0, has_side_effects=True, vmem_limit_bytes=VMEM_GRANT
         ),
     )(right_side, shift)
 

time: 46 us -> 45.9 us (level)
  no operation moved by 1% of the time
where the time goes in v2:
time: 45.9 us; the launch traced here: 45.7 us
  Pallas kernels  41.7 us (91%)
  local copies, waits for them, and re-layouts  3.3 us (7%)
  between operations  0.65 us (1%)
    pallas_call x1, Pallas kernels, on_device(): pl.pallas_call(functools.partial(kernel, gx, gy, X, Y, Z), out_shape=(sha...  41.7 us
    unnamed x6, local copies, waits for them, and re-layouts  3.3 us

profile of v2, /device:TPU:0, one launch (start us, length us, event | category | flops | bytes accessed | tf_op | source)
XLA Modules:
  0.0 45.7 jit_solution(12543873075301096140)
XLA Ops:
  0.6 0.0 copy-start
  0.6 0.9 %copy-done = f32[16,32,128]{2,1,0:T(8,128)S(1)} copy-done((f32[16,32,128]{2,1,0:T(8,128)S(1)}, f32[16,32,128]{2,1,0:T(8,128)}, u32[]{:S(2)}) %copy-start) | copy-done | bytes 262168
  1.6 0.0 copy-start.1
  1.6 0.9 %copy-done.1 = f32[16,32,128]{2,1,0:T(8,128)S(1)} copy-done((f32[16,32,128]{2,1,0:T(8,128)S(1)}, f32[16,32,128]{2,1,0:T(8,128)}, u32[]{:S(2)}) %copy-start.1) | copy-done | bytes 262168
  2.5 41.7 %shard_map.41 = (f32[16,32,128]{2,1,0:T(8,128)S(1)}, f32[16,32,128]{2,1,0:T(8,128)S(1)}) custom-call(f32[16,32,128]{2,1,0:T(8,128)S(1)} %copy-done, f32[16,32,128]{2,1,0:T(8,128)S(1)} %copy-done.1), custom_call_target="tpu_custom_call" | custom-call | tf_op jit(solution)/shard_map/pallas_call | solution.py:494
  44.3 0.7 %copy.6 = f32[16,32,128]{2,1,0:T(8,128)} copy(f32[16,32,128]{2,1,0:T(8,128)S(1)} %get-tuple-element.4) | data formatting | bytes 524288
  45.0 0.7 %copy.7 = f32[16,32,128]{2,1,0:T(8,128)} copy(f32[16,32,128]{2,1,0:T(8,128)S(1)} %get-tuple-element.5) | data formatting | bytes 524288
Async XLA Ops:
  0.6 1.0 %copy-start = (f32[16,32,128]{2,1,0:T(8,128)S(1)}, f32[16,32,128]{2,1,0:T(8,128)}, u32[]{:S(2)}) copy-start(f32[16,32,128]{2,1,0:T(8,128)} %rhs_hbm.1) | copy-start | bytes 786436
  1.6 0.9 %copy-start.1 = (f32[16,32,128]{2,1,0:T(8,128)S(1)}, f32[16,32,128]{2,1,0:T(8,128)}, u32[]{:S(2)}) copy-start(f32[16,32,128]{2,1,0:T(8,128)} %shf_hbm.1) | copy-start | bytes 786436

commit v3 on v2

--- a/solution.py
+++ b/solution.py
@@ -73,15 +73,6 @@
             barrier, inc=1, device_id=(xs[a], ys_at[b]), device_id_type=MESH
         )
 
-    for ref in (eA, eB, e1, vbox, vext, g0, dA, eAb, eBb, e1b, eAc, eBc, e1c):
-        lead = ref.shape[:-2]
-
-        def clear(i, ref=ref, lead=lead):
-            at = (i,) if len(lead) == 1 else (i // lead[1], lax.rem(i, lead[1]))
-            ref[at] = jnp.zeros(ref.shape[-2:], jnp.float32)
-
-        loop(lead[0] if len(lead) == 1 else lead[0] * lead[1], clear)
-
     for copy in loads:
         copy.wait()
 
@@ -90,9 +81,6 @@
             for q in range(2):
                 pack[side, p, 4 * q:4 * q + 2, :] = rhs[2 * p + q, at:at + 2, :]
                 pack[side, p, 4 * q + 2:4 * q + 4, :] = shf[2 * p + q, at:at + 2, :]
-
-    g0[2:X + 2, 3:Y + 3, :] = rhs[...]
-    dA[2:X + 2, 3:Y + 3, :] = shf[...]
 
     pl.semaphore_wait(barrier, n - 1)
 
@@ -174,6 +162,19 @@
 
     firsts = first_copies()
     start(firsts, is_sem, ir_sem)
+
+    for ref in (eA, eB, e1, vbox, vext, g0, dA, eAb, eBb, e1b, eAc, eBc, e1c):
+        lead = ref.shape[:-2]
+
+        def clear(i, ref=ref, lead=lead):
+            at = (i,) if len(lead) == 1 else (i // lead[1], lax.rem(i, lead[1]))
+            ref[at] = jnp.zeros(ref.shape[-2:], jnp.float32)
+
+        loop(lead[0] if len(lead) == 1 else lead[0] * lead[1], clear)
+
+    g0[2:X + 2, 3:Y + 3, :] = rhs[...]
+    dA[2:X + 2, 3:Y + 3, :] = shf[...]
+
 
     row = lax.broadcasted_iota(jnp.int32, (1, R, Z), 1)
     lane = lax.broadcasted_iota(jnp.int32, (1, R, Z), 2)
@@ -500,7 +501,7 @@
         compiler_params=pltpu.CompilerParams(
             collective_id=0, has_side_effects=True, vmem_limit_bytes=VMEM_GRANT
         ),
-    )(right_side, shift)
+    )(*(pltpu.with_memory_space_constraint(t, pltpu.HBM) for t in (right_side, shift)))
 
 
 def solution(mesh):

time: 45.9 us -> 42 us (0.915)
  Pallas kernels: 41.7 us -> 39.8 us
  local copies, waits for them, and re-layouts: 3.3 us -> 1.41 us
    pallas_call x1, Pallas kernels: 41.7 us -> 39.8 us  [on_device(): pl.pallas_call(functools.partial(kernel, gx, gy, X, Y, Z), out_shape=(sha...]
    unnamed x6 -> x2, local copies, waits for them, and re-layouts: 3.3 us -> 1.41 us
where the time goes in v3:
time: 42 us; the launch traced here: 41.8 us
  Pallas kernels  39.8 us (95%)
  local copies, waits for them, and re-layouts  1.41 us (3%)
  between operations  0.64 us (2%)
    pallas_call x1, Pallas kernels, on_device(): pl.pallas_call(functools.partial(kernel, gx, gy, X, Y, Z), out_shape=(sha...  39.8 us
    unnamed x2, local copies, waits for them, and re-layouts  1.41 us

profile of v3, /device:TPU:0, one launch (start us, length us, event | category | flops | bytes accessed | tf_op | source)
XLA Modules:
  0.0 41.8 jit_solution(9076636584263727168)
XLA Ops:
  0.6 39.8 %shard_map.41 = (f32[16,32,128]{2,1,0:T(8,128)S(1)}, f32[16,32,128]{2,1,0:T(8,128)S(1)}) custom-call(f32[16,32,128]{2,1,0:T(8,128)} %rhs_hbm.1, f32[16,32,128]{2,1,0:T(8,128)} %shf_hbm.1), custom_call_target="tpu_custom_call" | custom-call | tf_op jit(solution)/shard_map/pallas_call | solution.py:495
  40.4 0.7 %copy.6 = f32[16,32,128]{2,1,0:T(8,128)} copy(f32[16,32,128]{2,1,0:T(8,128)S(1)} %get-tuple-element.4) | data formatting | bytes 524288
  41.1 0.7 %copy.7 = f32[16,32,128]{2,1,0:T(8,128)} copy(f32[16,32,128]{2,1,0:T(8,128)S(1)} %get-tuple-element.5) | data formatting | bytes 524288

commit v4 on v3

--- a/solution.py
+++ b/solution.py
@@ -37,9 +37,9 @@
 def kernel(
     gx, gy, X, Y, Z,
     rhs_hbm, shf_hbm, out_x, out_r,
-    rhs, shf, g0, dA, wc0, cc0, e1, eA, eB, vbox, vext, wext,
+    rhs, shf, dA, wc0, cc0, e1, eA, eB, vbox, vext, wext,
     wc1, cc1, dd1, g1, e1b, eAb, eBb, wc2, cc2, g2, e1c, eAc, eBc,
-    pack, in_x, in_y, in_c, ypack, rx, ry, rc, gram,
+    partial, pack, in_x, in_y, in_c, ypack, rx, ry, rc, gram,
     ld_sem, is_sem, ir_sem, s_sem, r_sem, gs_sem, gr_sem,
 ):
     n = gx * gy
@@ -48,6 +48,7 @@
     ix, iy = lax.axis_index("gx"), lax.axis_index("gy")
     me = ix * gy + iy
     rows = slice(TOP, TOP + R)
+    g0 = wext.at[0]
 
     def there(dx, dy):
         ok = None
@@ -313,7 +314,7 @@
         ch = 4
 
         def body(i, sums):
-            w = own * wext[r, pl.ds(ch * i + 2, ch)]
+            w = own * wext[r + 1, pl.ds(ch * i + 2, ch)]
             terms = [own * g0[pl.ds(ch * i + 2, ch)] * vext[r, pl.ds(ch * i + 3, ch), rows, :]]
             terms += [vext[a, pl.ds(ch * i + 3, ch), rows, :] * w for a in range(r + 1)]
             return tuple(
@@ -321,12 +322,12 @@
             )
 
         zero = jnp.zeros((8, Z), jnp.float32)
-        return lax.fori_loop(0, X // ch, body, (zero,) * (r + 2))
+        done = lax.fori_loop(0, X // ch, body, (zero,) * (r + 2))
+        for k, t in enumerate(done):
+            partial[r * (r + 3) // 2 + k] = t
 
     scaled(e1, g0, wc0, n0, 4)
-    sums = []
-    for r in range(ROUNDS):
-        vcycle(vbox.at[r], g0 if r == 0 else wext.at[r - 1])
+    def exchange(r):
         d = depth(r)
         for i in range(n0):
             ypack[r, 0, d * i:d * i + d, :] = vbox[r, i + 1, TOP + 1:TOP + 1 + d, :]
@@ -346,7 +347,7 @@
 
         loop((n0 + 2) // 2, take)
         if r:
-            sums.append(dots(r - 1))
+            dots(r - 1)
 
         def use_back(dx, dy, got, slot):
             s = 5 - d if dx < 0 else X + 1
@@ -372,7 +373,7 @@
         def _():
             v[X + 3:X + 6, rows, :] = jnp.zeros((3, R, Z), jnp.float32)
 
-        w = wext.at[r]
+        w = wext.at[r + 1]
         last = r + 1 == ROUNDS
 
         def apply(i):
@@ -393,12 +394,19 @@
                     w[at:at + 2] = jnp.zeros((2, R, Z), jnp.float32)
                     e1[at + 1:at + 3, rows, :] = jnp.zeros((2, R, Z), jnp.float32)
 
-    sums.append(dots(ROUNDS - 1))
-    flat = [t for group in sums for t in group]
+    def one_round(now):
+        vcycle(vbox.at[now], wext.at[now])
+        for r in range(ROUNDS):
+            @pl.when(now == r)
+            def _(r=r):
+                exchange(r)
+
+    loop(ROUNDS, one_round)
+    dots(ROUNDS - 1)
     line = lax.broadcasted_iota(jnp.int32, (1, Z), 1)
     packed = jnp.zeros((1, Z), jnp.float32)
-    for k, s in enumerate(flat):
-        total = jnp.sum(jnp.sum(s, axis=0, keepdims=True), axis=1, keepdims=True)
+    for k in range(9):
+        total = jnp.sum(jnp.sum(partial[k], axis=0, keepdims=True), axis=1, keepdims=True)
         packed = jnp.where(line == k, total, packed)
     gram[me] = packed
 
@@ -441,10 +449,10 @@
         for j in range(4):
             p = 4 * i + j
             x = ys[0] * vext[0, p + 3, TOP + 3:TOP + Y + 3, :]
-            res = rhs[p] - ys[0] * wext[0, p + 2, 3:Y + 3, :]
+            res = rhs[p] - ys[0] * wext[1, p + 2, 3:Y + 3, :]
             for k in range(1, ROUNDS):
                 x = x + ys[k] * vext[k, p + 3, TOP + 3:TOP + Y + 3, :]
-                res = res - ys[k] * wext[k, p + 2, 3:Y + 3, :]
+                res = res - ys[k] * wext[k + 1, p + 2, 3:Y + 3, :]
             out_x[p] = x
             out_r[p] = res
 
@@ -476,11 +484,11 @@
     packed = up8(n0 * 5)
     scratch = [
         plain(X, Y), plain(X, Y),
-        field(n0), field(n0), field(n0), field(n0), tall(n0 + 2), tall(n0 + 2), tall(n0 + 2),
-        tall(ROUNDS, n0 + 2), tall(ROUNDS, n0 + 2), field(ROUNDS, n0),
+        field(n0), field(n0), field(n0), tall(n0 + 2), tall(n0 + 2), tall(n0 + 2),
+        tall(ROUNDS, n0 + 2), tall(ROUNDS, n0 + 2), field(ROUNDS + 1, n0),
         field(n1), field(n1), field(n1), field(n1), tall(n1 + 2), tall(n1 + 2), tall(n1 + 2),
         field(n2), field(n2), field(n2), tall(n2 + 2), tall(n2 + 2), tall(n2 + 2),
-        plain(2, X // 2, 8), plain(2, 2, 2, Y), plain(2, X // 2, 8), plain(4, 8),
+        plain(9, 8), plain(2, X // 2, 8), plain(2, 2, 2, Y), plain(2, X // 2, 8), plain(4, 8),
         plain(ROUNDS, 2, packed), field(ROUNDS, 2, 5), plain(ROUNDS, 2, packed),
         plain(ROUNDS, 4, 32), plain(n, 1),
         pltpu.SemaphoreType.DMA((2,)),

time: 42 us -> 42.1 us (level)
  no operation moved by 1% of the time
where the time goes in v4:
time: 42.1 us; the launch traced here: 41.9 us
  Pallas kernels  39.9 us (95%)
  local copies, waits for them, and re-layouts  1.41 us (3%)
  between operations  0.64 us (2%)
    pallas_call x1, Pallas kernels, on_device(): pl.pallas_call(functools.partial(kernel, gx, gy, X, Y, Z), out_shape=(sha...  39.9 us
    unnamed x2, local copies, waits for them, and re-layouts  1.41 us

profile of v4, /device:TPU:0, one launch (start us, length us, event | category | flops | bytes accessed | tf_op | source)
XLA Modules:
  0.0 41.9 jit_solution(4605828852363195629)
XLA Ops:
  0.6 39.9 %shard_map.41 = (f32[16,32,128]{2,1,0:T(8,128)S(1)}, f32[16,32,128]{2,1,0:T(8,128)S(1)}) custom-call(f32[16,32,128]{2,1,0:T(8,128)} %rhs_hbm.1, f32[16,32,128]{2,1,0:T(8,128)} %shf_hbm.1), custom_call_target="tpu_custom_call" | custom-call | tf_op jit(solution)/shard_map/pallas_call | solution.py:503
  40.5 0.7 %copy.6 = f32[16,32,128]{2,1,0:T(8,128)} copy(f32[16,32,128]{2,1,0:T(8,128)S(1)} %get-tuple-element.4) | data formatting | bytes 524288
  41.2 0.7 %copy.7 = f32[16,32,128]{2,1,0:T(8,128)} copy(f32[16,32,128]{2,1,0:T(8,128)S(1)} %get-tuple-element.5) | data formatting | bytes 524288
